TPU v7x, 256 devices: a whole 4x4x8 slice. The times are simulated.
256 devices in a mesh: occ: 8 (over z), vsec: 16 (over y, x_lo, core), aux: 2 (over x_hi).
Axes of the slice: x: 4 (x_hi: 2, x_lo: 2; x = x_hi * 2 + x_lo), y: 4, z: 8, core: 2. Of those that a mesh axis runs over, the one named last changes fastest.
Arguments:
- amplitudes: bfloat16 [128, 1024, 1024], P(('occ', 'vsec'), 'aux'), may hold values from -0.005859375 to 0.005859375
- left_factor: bfloat16 [4096, 32, 1024], P('aux', 'vsec'), may hold values from -0.75 to 0.75
- right_factor: bfloat16 [4096, 8, 1024], P('aux', None, 'occ'), may hold values from -0.75 to 0.75
- other_terms: float32 [128, 32, 8], P(('occ', 'aux'), 'vsec'), may hold values from -10.4 to 10.4
Outputs:
- residual: float32 [128, 32, 8], P(('occ', 'aux'), 'vsec')
- residual_norm: float32 [], replicated
All inputs are finite; a program needn't handle non-finite values.
Results may differ from a plain program's by a relative error of at most 0.002.
Values may be sent and summed in bfloat16 or wider, within the bound.
No kernel may reach another device: no remote copies, remote signals or barrier semaphores. Data moves between devices by JAX's collectives and lax.ppermute only.
A program may use at most 192 MiB of HBM per device.

v0:
```python
import functools

import jax
import jax.numpy as jnp
from jax import lax
from jax.sharding import Mesh
from jax.sharding import PartitionSpec as P

VSEC = ("vsec_0", "vsec_1", "vsec_2")
OCC_VSEC_AUX = ("occ", "vsec_0", "vsec_1", "vsec_2", "aux")
OCC_VSEC = ("occ", "vsec_0", "vsec_1", "vsec_2")


def split_up(x, dim, length):
    lengths = x.shape
    pieces = x.reshape(*lengths[:dim], length, lengths[dim] // length, *lengths[dim + 1 :])
    return jnp.moveaxis(pieces, dim, 0)


def sum_at_owner(x, axis, dim):
    pieces = split_up(x, dim, lax.axis_size(axis))
    arrived = lax.all_to_all(pieces, axis, split_axis=0, concat_axis=0, tiled=True)
    return arrived.sum(axis=0)


def by_axis(x, axes):
    return functools.reduce(lax.psum, axes, x)


def pair_order(ladder, sec_count, occ_count, per_device, arow_count, window):
    ordered = ladder.reshape(sec_count, occ_count, per_device, arow_count, window)
    return jnp.transpose(ordered, (1, 0, 2, 3, 4)).reshape(
        sec_count * occ_count * per_device, arow_count, window
    )


def on_device(amplitudes, left_factor, right_factor, other_terms):
    occ_count = lax.axis_size("occ")
    sec_count = lax.axis_size(VSEC)
    aux_rows, arow_count, virt_width = left_factor.shape
    window = right_factor.shape[1]
    slice_width = right_factor.shape[2]
    local_amps = lax.all_to_all(amplitudes, "occ", split_axis=2, concat_axis=0, tiled=True)
    pair_count = local_amps.shape[0]
    per_device = pair_count // occ_count
    partial_value = lax.dot_general(
        left_factor.reshape(aux_rows, arow_count * virt_width),
        right_factor.reshape(aux_rows, window * slice_width),
        (((0,), (0,)), ((), ())),
        preferred_element_type=jnp.float32,
    )
    partial_value = partial_value.reshape(arow_count, virt_width, window, slice_width)
    integral = lax.psum_scatter(partial_value, "aux", scatter_dimension=1, tiled=True).astype(
        jnp.bfloat16
    )
    amp_part = lax.all_to_all(local_amps, VSEC, split_axis=1, concat_axis=0, tiled=True)
    integral_part = lax.all_to_all(integral, VSEC, split_axis=1, concat_axis=0, tiled=True)
    partial_ladder = lax.dot_general(
        amp_part, integral_part, (((1, 2), (1, 3)), ((), ())), preferred_element_type=jnp.float32
    )
    all_rows = pair_order(
        partial_ladder, sec_count, occ_count, per_device, sec_count * arow_count, window
    )
    ordered = sum_at_owner(all_rows, VSEC, 1)
    summed = sum_at_owner(ordered, ("occ", "aux"), 0)
    residual = other_terms + summed
    squares = by_axis(jnp.sum(residual * residual), OCC_VSEC_AUX)
    return (residual, jnp.sqrt(squares))


def solution(mesh):
    torus = Mesh(
        mesh.devices.reshape(mesh.shape["occ"], 4, 2, 2, mesh.shape["aux"]),
        ("occ", "vsec_0", "vsec_1", "vsec_2", "aux"),
    )
    in_specs = (
        P(OCC_VSEC, "aux", None),
        P("aux", VSEC, None),
        P("aux", None, "occ"),
        P(("occ", "aux"), VSEC, None),
    )
    out_specs = (P(("occ", "aux"), VSEC, None), P())
    return jax.shard_map(
        on_device, mesh=torus, in_specs=in_specs, out_specs=out_specs, check_vma=False
    )
```

profile of v0, /device:TPU:1, one launch (start us, length us, event | category | flops | bytes accessed | tf_op | source)
XLA Modules:
  0.0 304.6 jit_solution(14689522687179588285)
XLA Ops:
  7.2 10.1 %copy.62 = bf16[256,8,2,1024]{3,1,2,0:T(8,128)(2,1)} copy(bf16[256,8,2,1024]{3,2,1,0:T(2,128)(2,1)} %bitcast.64) | data formatting | bytes 16777216
  17.3 12.3 %copy.43 = bf16[2048,2048]{1,0:T(8,128)(2,1)} copy(bf16[2048,2048]{0,1:T(8,128)(2,1)} %bitcast.61) | data formatting | bytes 16777216 | tf_op jit(solution)/shard_map/dot_general | solution.py:46
  29.6 5.3 %copy.70 = bf16[256,8,8,128]{3,1,2,0:T(8,128)(2,1)} copy(bf16[256,8,8,128]{3,2,1,0:T(8,128)(2,1)} %bitcast.70) | data formatting | bytes 8388608
  34.9 6.5 %copy.44 = bf16[1024,2048]{1,0:T(8,128)(2,1)} copy(bf16[1024,2048]{0,1:T(8,128)(2,1)} %bitcast.62) | data formatting | bytes 8388608 | tf_op jit(solution)/shard_map/dot_general | solution.py:46
  41.4 14.0 %fusion.2 = f32[2,1024,8,128]{3,1,2,0:T(8,128)} fusion(bf16[2,1024,2048,1]{2,1,3,0:T(8,128)(2,1)} %bitcast.65, bf16[8,128,2048,1]{2,1,0,3:T(8,128)(2,1)} %bitcast.71), kind=kOutput, calls=%fused_computation.7 | convolution fusion | flops 8589934592 | bytes 20971520 | tf_op jit(solution)/shard_map/dot_general | solution.py:46
  56.6 1.8 copy.47
  59.0 7.0 %reduce = bf16[1024,512]{1,0:T(8,128)(2,1)S(1)} reduce(bf16[1024,1,512]{2,1,0:T(2,128)(2,1)S(1)} %bitcast.67, bf16[]{:T(256)} %broadcast), dimensions={1}, to_apply=%bitcast.49.reduce_sub_computation | reduce | bytes 2097154
  67.6 9.0 %all-to-all-start.1 = ((bf16[8,2,32768]{2,1,0:T(2,128)(2,1)}), bf16[8,2,32768]{2,1,0:T(2,128)(2,1)S(1)}, u32[]{:S(2)}, u32[]{:S(2)}) async-start(bf16[8,2,32768]{2,1,0:T(2,128)(2,1)} %reshape.27), calls=%async_computation.2 | async-start | bytes 2097152 | tf_op jit(solution)/shard_map/all_to_all | solution.py:43
  76.6 88.5 %reduce-scatter.2.cloned.1.call-done = f32[2,512,8,128]{3,1,2,0:T(8,128)} async-done(((f32[2,1024,8,128]{3,1,2,0:T(8,128)}), f32[2,512,8,128]{3,1,2,0:T(8,128)}) %reduce-scatter.2.cloned.1.call-update) | async-done | bytes 4194320 | tf_op jit(solution)/shard_map/reduce_scatter | solution.py:53
  165.1 2.6 convert_element_type.3
  167.7 2.7 copy.45
  170.4 5.2 %all-to-all-start = ((bf16[2,512,8,128]{3,2,0,1:T(8,128)(2,1)}), bf16[2,512,8,128]{3,2,0,1:T(8,128)(2,1)}, u32[]{:S(2)}, u32[]{:S(2)}) async-start(bf16[2,512,8,128]{3,2,0,1:T(8,128)(2,1)} %copy.45), calls=%async_computation.1 | async-start | bytes 4194304 | tf_op jit(solution)/shard_map/all_to_all | solution.py:57
  178.4 24.2 %all-to-all-done = bf16[2,512,8,128]{3,2,0,1:T(8,128)(2,1)} async-done(((bf16[2,512,8,128]{3,2,0,1:T(8,128)(2,1)}), bf16[2,512,8,128]{3,2,0,1:T(8,128)(2,1)}, u32[]{:S(2)}, u32[]{:S(2)}) %all-to-all-start) | async-done | bytes 2097184 | tf_op jit(solution)/shard_map/all_to_all | solution.py:57
  202.6 4.4 %all-to-all-start.2 = ((bf16[8,512,128]{2,0,1:T(8,128)(2,1)}), bf16[8,512,128]{2,0,1:T(8,128)(2,1)S(1)}, u32[]{:S(2)}, u32[]{:S(2)}) async-start(bf16[8,512,128]{2,0,1:T(8,128)(2,1)} %copy.48), calls=%async_computation.3 | async-start | bytes 2097152 | tf_op jit(solution)/shard_map/all_to_all | solution.py:56
  207.0 2.1 copy.46
  209.1 13.7 %all-to-all-done.2 = bf16[8,512,128]{2,0,1:T(8,128)(2,1)S(1)} async-done(((bf16[8,512,128]{2,0,1:T(8,128)(2,1)}), bf16[8,512,128]{2,0,1:T(8,128)(2,1)S(1)}, u32[]{:S(2)}, u32[]{:S(2)}) %all-to-all-start.2) | async-done | bytes 1048608 | tf_op jit(solution)/shard_map/all_to_all | solution.py:56
  225.0 9.6 %all_to_all.64 = f32[16,128,2,8]{1,3,2,0:T(8,128)S(1)} all-to-all(f32[16,128,2,8]{1,3,2,0:T(8,128)S(1)} %bitcast.73), channel_id=1, replica_groups=mesh['occ'=8,'vsec_0'=4,'vsec_1'=2,'vsec_2'=2,'aux'=2] {'vsec_0','vsec_1..., dimensions={0} | all-to-all | bytes 262144 | tf_op jit(solution)/shard_map/all_to_all | solution.py:22
  235.5 8.3 %all-to-all-start.4 = ((f32[16,1,128]{2,1,0:T(1,128)}), f32[16,1,128]{2,1,0:T(1,128)S(1)}, u32[]{:S(2)}, u32[]{:S(2)}) async-start(f32[16,1,128]{2,1,0:T(1,128)} %reshape.29), calls=%async_computation.5 | async-start | bytes 16384 | tf_op jit(solution)/shard_map/all_to_all | solution.py:22
  243.9 8.7 %all-to-all-done.4 = f32[16,1,128]{2,1,0:T(1,128)S(1)} async-done(((f32[16,1,128]{2,1,0:T(1,128)}), f32[16,1,128]{2,1,0:T(1,128)S(1)}, u32[]{:S(2)}, u32[]{:S(2)}) %all-to-all-start.4) | async-done | bytes 8224 | tf_op jit(solution)/shard_map/all_to_all | solution.py:22
  254.6 11.6 %psum.35 = f32[]{:T(128)} all-reduce(f32[]{:T(128)} %get-tuple-element.4), channel_id=1, replica_groups=mesh['occ'=8,'vsec_0'=4,'vsec_1'=2,'vsec_2'=2,'aux'=2] {'occ'}, use_global_device_ids=true, to_apply=%region_4.0 | all-reduce | flops 1 | bytes 8 | tf_op jit(solution)/shard_map/psum | solution.py:27
  266.1 7.4 %psum.36 = f32[]{:T(128)} all-reduce(f32[]{:T(128)} %psum.35), channel_id=1, replica_groups=mesh['occ'=8,'vsec_0'=4,'vsec_1'=2,'vsec_2'=2,'aux'=2] {'vsec_0'}, use_global_device_ids=true, to_apply=%region_5.0 | all-reduce | flops 1 | bytes 8 | tf_op jit(solution)/shard_map/psum | solution.py:27
  273.5 4.7 %psum.37 = f32[]{:T(128)} all-reduce(f32[]{:T(128)} %psum.36), channel_id=1, replica_groups=mesh['occ'=8,'vsec_0'=4,'vsec_1'=2,'vsec_2'=2,'aux'=2] {'vsec_1'}, use_global_device_ids=true, to_apply=%region_6.0 | all-reduce | flops 1 | bytes 8 | tf_op jit(solution)/shard_map/psum | solution.py:27
  278.2 11.2 %psum.38 = f32[]{:T(128)} all-reduce(f32[]{:T(128)} %psum.37), channel_id=1, replica_groups=mesh['occ'=8,'vsec_0'=4,'vsec_1'=2,'vsec_2'=2,'aux'=2] {'vsec_2'}, use_global_device_ids=true, to_apply=%region_7.0 | all-reduce | flops 1 | bytes 8 | tf_op jit(solution)/shard_map/psum | solution.py:27
  290.0 5.9 %psum.39 = f32[]{:T(128)} all-reduce(f32[]{:T(128)} %psum.38), channel_id=1, replica_groups=mesh['occ'=8,'vsec_0'=4,'vsec_1'=2,'vsec_2'=2,'aux'=2] {'aux'}, use_global_device_ids=true, to_apply=%region_8.0 | all-reduce | flops 1 | bytes 8 | tf_op jit(solution)/shard_map/psum | solution.py:27
  (27 shorter events, 11.9 us)
Async XLA Ops:
  7.2 157.9 %reduce-scatter.2.cloned.1.call-start = ((), (), s32[]{:S(2)}) async-start(), calls=%async_computation.6 | async-start | bytes 12582912 | tf_op jit(solution)/shard_map/reduce_scatter | solution.py:53
  55.4 1.2 copy-start
  67.6 102.8 %all-to-all-start.1 = ((bf16[8,2,32768]{2,1,0:T(2,128)(2,1)}), bf16[8,2,32768]{2,1,0:T(2,128)(2,1)S(1)}, u32[]{:S(2)}, u32[]{:S(2)}) async-start(bf16[8,2,32768]{2,1,0:T(2,128)(2,1)} %reshape.27), calls=%async_computation.2 | async-start | bytes 2097152 | tf_op jit(solution)/shard_map/all_to_all | solution.py:43
  170.4 32.2 %all-to-all-start = ((bf16[2,512,8,128]{3,2,0,1:T(8,128)(2,1)}), bf16[2,512,8,128]{3,2,0,1:T(8,128)(2,1)}, u32[]{:S(2)}, u32[]{:S(2)}) async-start(bf16[2,512,8,128]{3,2,0,1:T(8,128)(2,1)} %copy.45), calls=%async_computation.1 | async-start | bytes 4194304 | tf_op jit(solution)/shard_map/all_to_all | solution.py:57
  202.6 20.2 %all-to-all-start.2 = ((bf16[8,512,128]{2,0,1:T(8,128)(2,1)}), bf16[8,512,128]{2,0,1:T(8,128)(2,1)S(1)}, u32[]{:S(2)}, u32[]{:S(2)}) async-start(bf16[8,512,128]{2,0,1:T(8,128)(2,1)} %copy.48), calls=%async_computation.3 | async-start | bytes 2097152 | tf_op jit(solution)/shard_map/all_to_all | solution.py:56
  209.1 34.7 %copy-start.1 = (f32[8,2,8]{2,1,0:T(2,128)S(1)}, f32[8,2,8]{2,1,0:T(2,128)}, u32[]{:S(2)}) copy-start(f32[8,2,8]{2,1,0:T(2,128)} %param.7) | copy-start | bytes 1540
  235.5 17.1 %all-to-all-start.4 = ((f32[16,1,128]{2,1,0:T(1,128)}), f32[16,1,128]{2,1,0:T(1,128)S(1)}, u32[]{:S(2)}, u32[]{:S(2)}) async-start(f32[16,1,128]{2,1,0:T(1,128)} %reshape.29), calls=%async_computation.5 | async-start | bytes 16384 | tf_op jit(solution)/shard_map/all_to_all | solution.py:22
Sparse Core Ops, SparseCore 0:
  55.6 109.5 reduce-scatter.1
where the time goes:
time: 306 us; the launch traced here: 305 us
  waiting for transfers between devices  135 us (44%)
  local copies, waits for them, and re-layouts  50.6 us (17%)
  blocking collectives  50.3 us (16%)
  starting transfers between devices  26.9 us (9%)
  between operations  16 us (5%)
  matrix products  14.7 us (5%)
  other arithmetic  10.9 us (4%)
    reduce_scatter x1, waiting for transfers between devices, on_device(): lax.psum_scatter(partial_value, 'aux', scatter_dimension=1, tiled=True)  88.5 us
    psum x5, blocking collectives, by_axis(): return functools.reduce(lax.psum, axes, x)  40.7 us
    all_to_all x1, waiting for transfers between devices, on_device(): lax.all_to_all(integral, VSEC, split_axis=1, concat_axis=0, tiled=True)  24.2 us
    unnamed x15, local copies, waits for them, and re-layouts  23.4 us
    dot_general x2, local copies, waits for them, and re-layouts, on_device(): lax.dot_general(left_factor.reshape(aux_rows, arow_count * virt_width), r...  18.8 us
    dot_general x1, matrix products, on_device(): lax.dot_general(left_factor.reshape(aux_rows, arow_count * virt_width), r...  14 us
    all_to_all x1, waiting for transfers between devices, on_device(): lax.all_to_all(local_amps, VSEC, split_axis=1, concat_axis=0, tiled=True)  13.7 us
    all_to_all x1, blocking collectives, sum_at_owner(): lax.all_to_all(pieces, axis, split_axis=0, concat_axis=0, tiled=True)  9.57 us
  transfers between devices with their start and end apart: 5, of which 4 were waited for; matrix products, arithmetic and copies ran while one was open for 7% of the time, Pallas kernels for 0%

commit v1 on v0

v1 whole, which is shorter than its diff:
```python
import jax
import jax.numpy as jnp
from jax import lax
from jax.sharding import Mesh
from jax.sharding import PartitionSpec as P

VSEC = ("vsec_0", "vsec_1", "vsec_2")
PLANE = ("aux",) + VSEC
OCC_VSEC = ("occ",) + VSEC
SCALE = 32.0


def exchange(x, axes):
    return lax.all_to_all(x, axes, split_axis=0, concat_axis=0, tiled=True)


def on_device(amplitudes, left_factor, right_factor, other_terms):
    occ_count = lax.axis_size("occ")
    aux_count = lax.axis_size("aux")
    sec_count = lax.axis_size(VSEC)
    plane_count = aux_count * sec_count
    aux_rows, arow_count, virt_width = left_factor.shape
    window, slice_width = right_factor.shape[1:]
    sub = virt_width // plane_count
    per_device = other_terms.shape[0]

    amps = amplitudes.reshape(sec_count, sub, occ_count, slice_width)
    amps = jnp.transpose(amps, (2, 0, 1, 3)).reshape(occ_count * sec_count, sub, slice_width)
    amps = exchange(amps, OCC_VSEC)

    partial = lax.dot_general(
        left_factor.reshape(aux_rows, arow_count * virt_width),
        right_factor.reshape(aux_rows, window * slice_width),
        (((0,), (0,)), ((), ())),
        preferred_element_type=jnp.float32,
    )
    partial = (partial * SCALE).astype(jnp.float16)
    partial = partial.reshape(arow_count, plane_count, sub, window, slice_width)
    partial = jnp.transpose(partial, (1, 0, 3, 2, 4))
    partial, amps = lax.optimization_barrier((partial, amps))
    arrived = exchange(partial, PLANE)
    halves = arrived.reshape(aux_count, sec_count * arow_count, window, sub, slice_width)
    integral = (halves.astype(jnp.float32).sum(axis=0) * (1.0 / SCALE)).astype(jnp.bfloat16)

    ladder = lax.dot_general(
        amps, integral, (((1, 2), (2, 3)), ((), ())), preferred_element_type=jnp.float32
    )
    ladder = ladder.reshape(occ_count, aux_count, per_device, sec_count, arow_count, window)
    ladder = jnp.transpose(ladder, (1, 3, 0, 2, 4, 5)).reshape(plane_count, -1, 128)
    mine = exchange(ladder, PLANE).sum(axis=0)
    mine = mine.reshape(occ_count, 1, 128)
    place = lax.axis_index("occ")
    slot = lax.broadcasted_iota(jnp.int32, (occ_count, 1, 128), 0)
    mine = mine + jnp.where(slot == place, other_terms.reshape(1, 1, 128), 0.0)
    spread = jnp.broadcast_to(mine.reshape(1, occ_count, 128), (occ_count, occ_count, 128))
    whole = exchange(spread, "occ").sum(axis=0)
    residual = lax.dynamic_slice_in_dim(whole, place, 1, 0).reshape(other_terms.shape)
    square = jnp.sum(whole * whole)
    squares = exchange(jnp.broadcast_to(square, (plane_count, 1, 128)), PLANE)
    norm = jnp.sqrt(jnp.sum(squares[:, 0, 0]))
    return (residual, norm)


def solution(mesh):
    torus = Mesh(
        mesh.devices.reshape(mesh.shape["occ"], 4, 2, 2, mesh.shape["aux"]),
        ("occ", "vsec_0", "vsec_1", "vsec_2", "aux"),
    )
    in_specs = (
        P(OCC_VSEC, "aux", None),
        P("aux", VSEC, None),
        P("aux", None, "occ"),
        P(("occ", "aux"), VSEC, None),
    )
    out_specs = (P(("occ", "aux"), VSEC, None), P())
    return jax.shard_map(
        on_device, mesh=torus, in_specs=in_specs, out_specs=out_specs, check_vma=False
    )
```

time: 306 us -> 157 us (0.51)
  waiting for transfers between devices: 135 us -> 15 us
  local copies, waits for them, and re-layouts: 50.6 us -> 26.6 us
  blocking collectives: 50.3 us -> 69.6 us
  between operations: 16 us -> 2.59 us
  other arithmetic: 10.9 us -> 3.13 us
    reduce_scatter x1 -> x0, waiting for transfers between devices: 88.5 us -> none  [on_device(): lax.psum_scatter(partial_value, 'aux', scatter_dimension=1, tiled=True)]
    all_to_all x1 -> x2, blocking collectives: 9.57 us -> 69.6 us  [exchange(): return lax.all_to_all(x, axes, split_axis=0, concat_axis=0, tiled=True)]
    psum x5 -> x0, blocking collectives: 40.7 us -> none  [by_axis(): return functools.reduce(lax.psum, axes, x)]
    all_to_all x4 -> x3, waiting for transfers between devices: 46.6 us -> 15 us  [exchange(): return lax.all_to_all(x, axes, split_axis=0, concat_axis=0, tiled=True)]
    dot_general x3 -> x1, local copies, waits for them, and re-layouts: 19.1 us -> 0.08 us  [on_device(): lax.dot_general(amps, integral, (((1, 2), (2, 3)), ((), ())), preferred_e...]
    unnamed x15 -> x5, local copies, waits for them, and re-layouts: 23.4 us -> 13 us
    reshape x2 -> x6, local copies, waits for them, and re-layouts: 0.14 us -> 9.99 us  [the longest x1 3.48 us: on_device(): partial = partial.reshape(arow_count, plane_count, sub, window, slice_width)]
    unnamed x1 -> x0, other arithmetic: 7.04 us -> none
  transfers between devices with their start and end apart: 5 -> 3, of which waited for: 4 -> 3; matrix products, arithmetic and copies ran while one was open for 7% -> 18% of each run, Pallas kernels for 0% -> 0%
where the time goes in v1:
time: 157 us; the launch traced here: 156 us
  blocking collectives  69.6 us (44%)
  local copies, waits for them, and re-layouts  26.6 us (17%)
  starting transfers between devices  25 us (16%)
  waiting for transfers between devices  15 us (10%)
  matrix products  14.2 us (9%)
  other arithmetic  3.13 us (2%)
  between operations  2.59 us (2%)
    all_to_all x2, blocking collectives, exchange(): return lax.all_to_all(x, axes, split_axis=0, concat_axis=0, tiled=True)  69.6 us
    all_to_all x3, starting transfers between devices, exchange(): return lax.all_to_all(x, axes, split_axis=0, concat_axis=0, tiled=True)  25 us
    all_to_all x3, waiting for transfers between devices, exchange(): return lax.all_to_all(x, axes, split_axis=0, concat_axis=0, tiled=True)  15 us
    unnamed x5, local copies, waits for them, and re-layouts  13 us
    dot_general x1, matrix products, on_device(): lax.dot_general(left_factor.reshape(aux_rows, arow_count * virt_width), r...  12.7 us
    reshape x1, local copies, waits for them, and re-layouts, on_device(): partial = partial.reshape(arow_count, plane_count, sub, window, slice_width)  3.48 us
    reshape x1, local copies, waits for them, and re-layouts, on_device(): ladder.reshape(occ_count, aux_count, per_device, sec_count, arow_count, w...  3.16 us
  transfers between devices with their start and end apart: 3, of which 3 were waited for; matrix products, arithmetic and copies ran while one was open for 18% of the time, Pallas kernels for 0%

profile of v1, /device:TPU:1, one launch (start us, length us, event | category | flops | bytes accessed | tf_op | source)
XLA Modules:
  0.0 156.1 jit_solution(9934835329607633933)
XLA Ops:
  0.6 1.5 copy.38
  2.1 1.3 copy.26
  3.4 14.9 %all-to-all-start = ((bf16[128,32,128]{2,1,0:T(8,128)(2,1)}), bf16[128,32,128]{2,1,0:T(8,128)(2,1)S(1)}, u32[]{:S(2)}, u32[]{:S(2)}) async-start(bf16[128,32,128]{2,1,0:T(8,128)(2,1)} %bitcast.2), calls=%async_computation | async-start | bytes 2097152 | tf_op jit(solution)/shard_map/all_to_all | solution.py:14
  18.3 10.1 %copy.35 = bf16[256,8,2,1024]{3,1,2,0:T(8,128)(2,1)} copy(bf16[256,8,2,1024]{3,2,1,0:T(2,128)(2,1)} %bitcast.41) | data formatting | bytes 16777216
  28.4 12.7 %fusion.2 = f16[256,8,8,128]{3,1,2,0:T(8,128)(2,1)S(1)} fusion(bf16[2048,2048]{1,0:T(8,128)(2,1)} %bitcast.42, bf16[256,8,8,128]{3,2,1,0:T(8,128)(2,1)} %bitcast.46), kind=kOutput, calls=%fused_computation.6 | convolution fusion | flops 8594128896 | bytes 16777216 | tf_op jit(solution)/shard_map/dot_general | solution.py:31
  41.1 1.4 copy.37
  42.5 3.5 %copy.54 = f16[2,32,32,8,128]{4,2,3,0,1:T(8,128)(2,1)} copy(f16[2,32,32,8,128]{4,3,2,1,0:T(8,128)(2,1)S(1)} %bitcast.39) | data formatting | bytes 8388608 | tf_op jit(solution)/shard_map/reshape | solution.py:38
  46.0 1.3 all-to-all-done
  47.3 57.2 %all_to_all.25 = f16[32,2,8,32,128]{4,3,2,1,0:T(8,128)(2,1)S(1)} all-to-all(f16[32,2,8,32,128]{4,3,2,1,0:T(8,128)(2,1)} %bitcast.38), channel_id=1, replica_groups=mesh['occ'=8,'vsec_0'=4,'vsec_1'=2,'vsec_2'=2,'aux'=2] {'aux','vsec_0','..., dimensions={0} | all-to-all | bytes 8388608 | tf_op jit(solution)/shard_map/all_to_all | solution.py:14
  104.5 1.2 convert_reduce_fusion
  106.3 1.5 fusion.7
  107.8 3.2 %reshape.76 = f32[8,2,8,16,2,8]{2,1,0,5,4,3:T(2,128)S(1)} reshape(f32[128,32,8]{0,2,1:T(8,128)S(1)} %copy.29) | data formatting | bytes 262144 | tf_op jit(solution)/shard_map/reshape | solution.py:48
  111.0 2.1 %copy.30 = f32[2,16,8,8,2,8]{1,0,5,4,3,2:T(2,128)S(1)} copy(f32[2,16,8,8,2,8]{3,0,2,5,4,1:T(2,128)S(1)} %bitcast.43) | data formatting | bytes 262144 | tf_op jit(solution)/shard_map/transpose | solution.py:49
  113.1 0.6 reshape.77
  113.7 0.8 copy.31
  114.5 4.4 %all-to-all-start.2 = ((f32[32,8,128]{2,1,0:T(8,128)}), f32[32,8,128]{2,1,0:T(8,128)S(1)}, u32[]{:S(2)}, u32[]{:S(2)}) async-start(f32[32,8,128]{2,1,0:T(8,128)} %copy.31), calls=%async_computation.2 | async-start | bytes 262144 | tf_op jit(solution)/shard_map/all_to_all | solution.py:14
  119.0 7.4 %all-to-all-done.2 = f32[32,8,128]{2,1,0:T(8,128)S(1)} async-done(((f32[32,8,128]{2,1,0:T(8,128)}), f32[32,8,128]{2,1,0:T(8,128)S(1)}, u32[]{:S(2)}, u32[]{:S(2)}) %all-to-all-start.2) | async-done | bytes 131104 | tf_op jit(solution)/shard_map/all_to_all | solution.py:14
  126.5 12.5 %all_to_all.26 = f32[8,8,128]{2,1,0:T(8,128)S(1)} all-to-all(f32[8,8,128]{2,1,0:T(8,128)S(1)} %broadcast_in_dim.25), channel_id=1, replica_groups=mesh['occ'=8,'vsec_0'=4,'vsec_1'=2,'vsec_2'=2,'aux'=2] {'occ'}, dimensions={0} | all-to-all | bytes 65536 | tf_op jit(solution)/shard_map/all_to_all | solution.py:14
  139.0 0.6 multiply_reduce_fusion
  139.6 1.2 broadcast_in_dim.26
  140.9 5.7 %all-to-all-start.4 = ((f32[32,1,128]{2,1,0:T(1,128)}), f32[32,1,128]{2,1,0:T(1,128)S(1)}, u32[]{:S(2)}, u32[]{:S(2)}) async-start(f32[32,1,128]{2,1,0:T(1,128)} %broadcast_in_dim.26), calls=%async_computation.4 | async-start | bytes 32768 | tf_op jit(solution)/shard_map/all_to_all | solution.py:14
  146.6 0.7 reshape.78
  147.3 6.3 %all-to-all-done.4 = f32[32,1,128]{2,1,0:T(1,128)S(1)} async-done(((f32[32,1,128]{2,1,0:T(1,128)}), f32[32,1,128]{2,1,0:T(1,128)S(1)}, u32[]{:S(2)}, u32[]{:S(2)}) %all-to-all-start.4) | async-done | bytes 16416 | tf_op jit(solution)/shard_map/all_to_all | solution.py:14
  153.7 0.6 slice_reduce_fusion
  (11 shorter events, 0.9 us)
Async XLA Ops:
  3.4 43.9 %all-to-all-start = ((bf16[128,32,128]{2,1,0:T(8,128)(2,1)}), bf16[128,32,128]{2,1,0:T(8,128)(2,1)S(1)}, u32[]{:S(2)}, u32[]{:S(2)}) async-start(bf16[128,32,128]{2,1,0:T(8,128)(2,1)} %bitcast.2), calls=%async_computation | async-start | bytes 2097152 | tf_op jit(solution)/shard_map/all_to_all | solution.py:14
  107.7 11.2 %copy-start = (f32[8,2,8]{2,1,0:T(2,128)S(1)}, f32[8,2,8]{2,1,0:T(2,128)}, u32[]{:S(2)}) copy-start(f32[8,2,8]{2,1,0:T(2,128)} %param.7) | copy-start | bytes 1540
  114.5 11.9 %all-to-all-start.2 = ((f32[32,8,128]{2,1,0:T(8,128)}), f32[32,8,128]{2,1,0:T(8,128)S(1)}, u32[]{:S(2)}, u32[]{:S(2)}) async-start(f32[32,8,128]{2,1,0:T(8,128)} %copy.31), calls=%async_computation.2 | async-start | bytes 262144 | tf_op jit(solution)/shard_map/all_to_all | solution.py:14
  140.9 12.8 %all-to-all-start.4 = ((f32[32,1,128]{2,1,0:T(1,128)}), f32[32,1,128]{2,1,0:T(1,128)S(1)}, u32[]{:S(2)}, u32[]{:S(2)}) async-start(f32[32,1,128]{2,1,0:T(1,128)} %broadcast_in_dim.26), calls=%async_computation.4 | async-start | bytes 32768 | tf_op jit(solution)/shard_map/all_to_all | solution.py:14
